TPU v7x, 32 devices: a whole 2x2x4 slice. The times are simulated.
32 devices in a mesh: lat: 4 (over z), lon: 8 (over y, x, core).
Axes of the slice: x: 2, y: 2, z: 4, core: 2. Of those that a mesh axis runs over, the one named last changes fastest.
Arguments:
- poleward_flow: float32 [10, 4, 256, 1024], P(None, None, 'lat', 'lon'), may hold values from -16 to 16
- potential_warmth: float32 [10, 4, 256, 1024], P(None, None, 'lat', 'lon'), may hold values from -16 to 16
- water_profile_flag: int32 [256, 1024], P('lat', 'lon'), may hold values from 0 to 1
- floor_count: int32 [256, 1024], P('lat', 'lon'), may hold values from 0 to 4, as said below
- catchment_label_for_site: int32 [256, 1024], P('lat', 'lon'), may hold values from 0 to 9
Outputs:
- eddy_temp: float32 [4, 256, 1024], P(None, 'lat', 'lon')
- transport: float32 [4, 10, 4, 256], P(None, None, None, ('lat', 'lon'))
Inputs may be any that keep to these rules, and one draw needn't show every extreme that they name: `floor_count`: land rows of zeros occur at some latitudes; elsewhere columns have 1 to 4 wet levels.
All inputs are finite; a program needn't handle non-finite values.
Results may differ from a plain program's by a relative error of at most 0.0003.
Values sent between devices are 32-bit elements; how exact they have to be, the bound alone decides.
A program may use at most 64 MiB of HBM per device.

v0:
```python
import functools
import math

import jax
import jax.numpy as jnp
from jax import lax
from jax.experimental import pallas as pl
from jax.experimental.pallas import tpu as pltpu
from jax.sharding import PartitionSpec as P

BASINS = 10
MESH = pl.DeviceIdType.MESH
SUB = 8
LANES = 128


def kernel(
    lat_devices, lon_devices, snapshots, levels, share_rows,
    flow_hbm, warmth_hbm, flag_hbm, floor_hbm, label_hbm,
    eddy_ref, transport_ref,
    flag_ref, floor_ref, label_ref, depth, flow, warmth, average, dots,
    halo_out, halo_in, stats, received, sums, pair_sums, chip_sums, peer_sums, peer_last,
    load_flow, load_warmth, load_columns, halo_send, halo_recv,
    stat_send, stat_recv, pair_send, pair_recv, sum_send, sum_recv, last_send, last_recv,
):
    rows = flow.shape[1]
    blocks = rows // SUB
    last = blocks - 1
    owners = SUB // share_rows
    planes = snapshots * levels
    packed = stats.shape[1]
    fields = dots.shape[1] // SUB
    used = BASINS * SUB
    lat = lax.axis_index("lat")
    me = lax.axis_index("lon")
    own_block = me // owners
    scaling = 1.0 / math.sqrt(LANES * lon_devices)

    def window(b):
        return pl.ds(pl.multiple_of(b * SUB, SUB), SUB)

    def flow_copy(b):
        at = window(b)
        return pltpu.make_async_copy(flow_hbm.at[:, at, :], flow.at[:, at, :], load_flow.at[b])

    def warmth_copy(b):
        at = window(b)
        return pltpu.make_async_copy(warmth_hbm.at[:, at, :], warmth.at[:, at, :], load_warmth.at[b])

    columns = [
        pltpu.make_async_copy(src, dst, load_columns.at[n])
        for n, (src, dst) in enumerate(
            ((flag_hbm, flag_ref), (floor_hbm, floor_ref), (label_hbm, label_ref))
        )
    ]
    for copy in columns:
        copy.start()
    for b in range(blocks):
        warmth_copy(b).start()
        flow_copy(b).start()

    barrier = pltpu.get_barrier_semaphore()

    def greet(d, carry):
        pl.semaphore_signal(
            barrier, inc=1, device_id=(lat, lax.rem(me + d, lon_devices)), device_id_type=MESH
        )
        return carry

    @pl.when(lat > 0)
    def _():
        pl.semaphore_signal(barrier, inc=1, device_id=(lat - 1, me), device_id_type=MESH)

    @pl.when(lat < lat_devices - 1)
    def _():
        pl.semaphore_signal(barrier, inc=1, device_id=(lat + 1, me), device_id_type=MESH)

    lax.fori_loop(1, lon_devices, greet, 0)

    halo_copy = pltpu.make_async_remote_copy(
        src_ref=halo_out, dst_ref=halo_in, send_sem=halo_send, recv_sem=halo_recv,
        device_id=(jnp.maximum(lat - 1, 0), me), device_id_type=MESH,
    )

    chips = lon_devices // 2
    core = lax.rem(me, 2)
    pair_copy = pltpu.make_async_remote_copy(
        src_ref=sums.at[pl.ds(0, last)], dst_ref=pair_sums, send_sem=pair_send, recv_sem=pair_recv,
        device_id=(lat, me + 1 - 2 * core), device_id_type=MESH,
    )

    def chip_copy(to, source):
        return pltpu.make_async_remote_copy(
            src_ref=chip_sums, dst_ref=peer_sums.at[source],
            send_sem=sum_send.at[to], recv_sem=sum_recv.at[source],
            device_id=(lat, 2 * to + core), device_id_type=MESH,
        )

    def last_copy(to, source):
        return pltpu.make_async_remote_copy(
            src_ref=sums.at[last], dst_ref=peer_last.at[source],
            send_sem=last_send.at[to], recv_sem=last_recv.at[source],
            device_id=(lat, to), device_id_type=MESH,
        )

    def each_chip(action):
        def step(d, carry):
            action(lax.rem(me // 2 + d, chips))
            return carry

        lax.fori_loop(1, chips, step, 0)

    def stat_copy(b, to, source):
        return pltpu.make_async_remote_copy(
            src_ref=stats.at[b], dst_ref=received.at[source],
            send_sem=stat_send.at[to], recv_sem=stat_recv.at[source],
            device_id=(lat, to), device_id_type=MESH,
        )

    def each_peer(action):
        def step(d, carry):
            action(lax.rem(me + d, lon_devices))
            return carry

        lax.fori_loop(1, lon_devices, step, 0)

    sub = lax.broadcasted_iota(jnp.int32, (SUB, LANES), 0)
    level = lax.broadcasted_iota(jnp.int32, (levels, SUB, LANES), 0).astype(jnp.float32)

    def next_row(here, after):
        first = lax.broadcasted_iota(jnp.int32, here.shape, here.ndim - 2) == 0
        return pltpu.roll(jnp.where(first, after, here), SUB - 1, here.ndim - 2)

    def both_halves(x):
        return x + pltpu.roll(x, levels, 0)

    def wet_cells(b):
        here = depth[window(b), :]
        limit = jnp.minimum(here, next_row(here, depth[window(b + 1), :]))
        return (level < limit[None]).astype(jnp.float32)

    def block_stats(b, carry):
        at = window(b)
        wet = wet_cells(b)
        velocity = flow[:, at, :].reshape(snapshots, levels, SUB, LANES)
        here = warmth[:, at, :]
        point = (0.5 * (here + next_row(here, warmth[:, window(b + 1), :]))).reshape(
            snapshots, levels, SUB, LANES
        )
        mean_velocity = jnp.sum(velocity, axis=0) * (1.0 / snapshots)
        mean_warmth = jnp.sum(point, axis=0) * (1.0 / snapshots)
        cross = jnp.sum((velocity - mean_velocity) * (point - mean_warmth), axis=0) * (1.0 / snapshots)
        average[:, at, :] = mean_warmth
        values = jnp.concatenate(
            [
                (velocity * wet[None]).reshape(planes, SUB, LANES),
                (point * wet[None]).reshape(planes, SUB, LANES),
                wet,
                wet,
                mean_velocity * mean_warmth * wet,
                cross * wet,
            ],
            axis=0,
        ).reshape(-1, LANES)
        high = values.astype(jnp.bfloat16)
        low = (values - high.astype(jnp.float32)).astype(jnp.bfloat16)
        labels = label_ref[at, :]
        member = jnp.concatenate(
            [(labels == n).astype(jnp.float32) for n in range(LANES // SUB)], axis=0
        ).astype(jnp.bfloat16)
        dots[b] = lax.dot_general(
            jnp.concatenate([high, low], axis=1), jnp.concatenate([member, member], axis=1),
            (((1,), (1,)), ((), ())), preferred_element_type=jnp.float32,
        )
        row_of = lax.rem(lax.broadcasted_iota(jnp.int32, (fields, LANES), 1), SUB)
        zonal = dots[b, pl.ds(0, fields, stride=SUB), :]
        for j in range(1, SUB):
            zonal = jnp.where(row_of == j, dots[b, pl.ds(j, fields, stride=SUB), :], zonal)
        warmth_sum = both_halves(
            jnp.sum(zonal[planes : 2 * planes].reshape(planes // SUB, SUB, LANES), axis=0)
        )
        count = zonal[2 * planes : 2 * planes + SUB]
        sums[pl.ds(b, 1)] = jnp.where(sub < levels, warmth_sum, count)[None]
        half = packed // 2
        rest = zonal[packed:]
        spare = lax.broadcasted_iota(jnp.int32, (half, LANES), 1) >= used
        stats[pl.ds(b, 1)] = jnp.concatenate(
            [
                jnp.where(spare, pltpu.roll(rest, used, 1), zonal[:half]),
                jnp.where(spare, pltpu.roll(rest, 2 * used - LANES, 1), zonal[half:packed]),
            ],
            axis=0,
        )[None]
        return carry

    for copy in columns:
        copy.wait()
    depth[pl.ds(0, rows), :] = (flag_ref[...] * floor_ref[...]).astype(jnp.float32)
    for b in range(blocks):
        warmth_copy(b).wait()
    halo_out[pl.ds(0, planes), :] = warmth[:, 0, :]
    halo_out[pl.ds(planes, SUB), :] = depth[pl.ds(0, SUB), :]

    def early_block(b, carry):
        flow_copy(b).wait()
        return block_stats(b, carry)

    for b in range(blocks):
        flow_copy(b).wait()
    for b in range(last // 2):
        block_stats(b, 0)

    pl.semaphore_wait(
        barrier,
        lon_devices - 1 + (lat > 0).astype(jnp.int32) + (lat < lat_devices - 1).astype(jnp.int32),
    )

    @pl.when(lat > 0)
    def _():
        halo_copy.start()

    def send_stats(low, high, to):
        @pl.when(jnp.logical_and(to // owners >= low, to // owners < high))
        def _():
            stat_copy(to // owners, to, me).start()

    each_peer(functools.partial(send_stats, 0, last // 2))
    for b in range(last // 2, last):
        block_stats(b, 0)
    pair_copy.start()

    each_peer(functools.partial(send_stats, last // 2, last))
    pair_copy.wait_recv()
    chip_sums[...] = sums[pl.ds(0, last)] + pair_sums[...]
    each_chip(lambda to: chip_copy(to, me // 2).start())

    @pl.when(lat < lat_devices - 1)
    def _():
        halo_copy.wait_recv()
        warmth[:, rows, :] = halo_in[pl.ds(0, planes), :]
        depth[pl.ds(rows, SUB), :] = halo_in[pl.ds(planes, SUB), :]

    @pl.when(lat == lat_devices - 1)
    def _():
        warmth[:, rows, :] = jnp.zeros((planes, LANES), jnp.float32)
        depth[pl.ds(rows, SUB), :] = jnp.zeros((SUB, LANES), jnp.float32)

    block_stats(last, 0)
    each_peer(lambda to: last_copy(to, me).start())

    def send_last(to):
        @pl.when(to // owners == last)
        def _():
            stat_copy(last, to, me).start()

    each_peer(send_last)

    def block_eddy(b, block_sums):
        at = pl.ds(b * SUB, SUB)
        wet = wet_cells(b)
        index = label_ref[at, :] * SUB + sub
        bar = block_sums / jnp.maximum(pltpu.roll(block_sums, levels, 0), 1.0) * (1.0 / snapshots)
        for k in range(levels):
            cells = jnp.take_along_axis(
                jnp.broadcast_to(bar[k : k + 1], (SUB, LANES)), index, axis=1
            )
            eddy_ref[k, at, :] = wet[k] * (average[k, at, :] - cells)

    def add_sums(d, total):
        source = lax.rem(me // 2 + chips - d, chips)
        chip_copy(0, source).wait_recv()
        return total + peer_sums[pl.ds(source, 1)][0]

    first_sums = lax.fori_loop(1, chips, add_sums, chip_sums[...])
    for b in range(last):
        block_eddy(b, first_sums[b])

    def add_received(d, total):
        source = lax.rem(me + lon_devices - d, lon_devices)
        stat_copy(0, me, source).wait_recv()
        return total + received[pl.ds(source, 1)][0]

    total = lax.fori_loop(1, lon_devices, add_received, stats[pl.ds(own_block, 1)][0])
    half = packed // 2
    lane = lax.broadcasted_iota(jnp.int32, (half, LANES), 1)
    total = jnp.concatenate(
        [
            total,
            jnp.where(
                lane < LANES - used,
                pltpu.roll(total[:half], LANES - used, 1),
                pltpu.roll(total[half:], 2 * LANES - 2 * used, 1),
            ),
        ],
        axis=0,
    )
    count = total[2 * planes : 2 * planes + SUB]
    divisor = jnp.maximum(count, 1.0)
    means_v = total[:planes].reshape(planes // SUB, SUB, LANES) / divisor
    means_t = total[planes : 2 * planes].reshape(planes // SUB, SUB, LANES) / divisor
    bar_v = both_halves(jnp.sum(means_v, axis=0)) * (1.0 / snapshots)
    bar_t = both_halves(jnp.sum(means_t, axis=0)) * (1.0 / snapshots)
    swing = both_halves(jnp.sum((means_v - bar_v) * (means_t - bar_t), axis=0)) * (1.0 / snapshots)
    upper = jnp.where(sub < levels, scaling * count * bar_v * bar_t, scaling * count * swing)
    lower = scaling * total[2 * planes + SUB : 2 * planes + 2 * SUB] - upper
    if owners > 1:
        shift = LANES - lax.rem(me, owners) * share_rows
        upper = pltpu.roll(upper, shift, 1)
        lower = pltpu.roll(lower, shift, 1)
    spread = lax.rem(lax.broadcasted_iota(jnp.int32, (SUB, LANES), 1) * SUB + sub, LANES)
    for c, part in enumerate((upper, lower, upper, lower)):
        for k in range(levels):
            row = c // 2 * levels + k
            table = jnp.take_along_axis(
                jnp.broadcast_to(part[row : row + 1], (SUB, LANES)), spread, axis=1
            )
            transport_ref[c, k] = table[:share_rows, :BASINS]

    def add_last(d, total):
        source = lax.rem(me + lon_devices - d, lon_devices)
        last_copy(0, source).wait_recv()
        return total + peer_last[pl.ds(source, 1)][0]

    block_eddy(last, lax.fori_loop(1, lon_devices, add_last, sums[last]))

    @pl.when(lat > 0)
    def _():
        halo_copy.wait_send()

    pair_copy.wait_send()
    each_chip(lambda to: chip_copy(to, me // 2).wait_send())

    def sent(to):
        last_copy(to, me).wait_send()
        stat_copy(to // owners, to, me).wait_send()

    each_peer(sent)


def shards(
    lat_devices, lon_devices,
    poleward_flow, potential_warmth, water_profile_flag, floor_count, catchment_label_for_site,
):
    snapshots, levels, rows, columns = poleward_flow.shape
    share_rows = rows // lon_devices
    blocks = rows // SUB
    planes = snapshots * levels
    fields = 2 * planes + 4 * levels
    packed = fields * 2 // 3
    f32, i32, vmem, dma = jnp.float32, jnp.int32, pltpu.VMEM, pltpu.SemaphoreType.DMA
    eddy_temp, transport = pl.pallas_call(
        functools.partial(kernel, lat_devices, lon_devices, snapshots, levels, share_rows),
        out_shape=(
            vmem((levels, rows, columns), f32),
            vmem((4, levels, share_rows, BASINS), f32),
        ),
        in_specs=[pl.BlockSpec(memory_space=pltpu.HBM)] * 5,
        out_specs=(pl.BlockSpec(memory_space=vmem), pl.BlockSpec(memory_space=vmem)),
        scratch_shapes=[
            vmem((rows, columns), i32),
            vmem((rows, columns), i32),
            vmem((rows, columns), i32),
            vmem((rows + SUB, columns), f32),
            vmem((planes, rows, columns), f32),
            vmem((planes, rows + SUB, columns), f32),
            vmem((levels, rows, columns), f32),
            vmem((blocks, fields * SUB, LANES), f32),
            vmem((planes + SUB, LANES), f32),
            vmem((planes + SUB, LANES), f32),
            vmem((blocks, packed, LANES), f32),
            vmem((lon_devices, packed, LANES), f32),
            vmem((blocks, SUB, LANES), f32),
            vmem((blocks - 1, SUB, LANES), f32),
            vmem((blocks - 1, SUB, LANES), f32),
            vmem((lon_devices // 2, blocks - 1, SUB, LANES), f32),
            vmem((lon_devices, SUB, LANES), f32),
            dma((blocks,)),
            dma((blocks,)),
            dma((3,)),
            dma,
            dma,
            dma((lon_devices,)),
            dma((lon_devices,)),
            dma,
            dma,
            dma((lon_devices // 2,)),
            dma((lon_devices // 2,)),
            dma((lon_devices,)),
            dma((lon_devices,)),
        ],
        compiler_params=pltpu.CompilerParams(
            collective_id=0, has_side_effects=True, vmem_limit_bytes=62 * 1024 * 1024
        ),
        name="heat_transport",
    )(
        poleward_flow.reshape(planes, rows, columns),
        potential_warmth.reshape(planes, rows, columns),
        water_profile_flag,
        floor_count,
        catchment_label_for_site,
    )
    return eddy_temp, jnp.transpose(transport, (0, 3, 1, 2))


def solution(mesh):
    return jax.shard_map(
        functools.partial(shards, mesh.shape["lat"], mesh.shape["lon"]),
        mesh=mesh,
        in_specs=(
            P(None, None, "lat", "lon"),
            P(None, None, "lat", "lon"),
            P("lat", "lon"),
            P("lat", "lon"),
            P("lat", "lon"),
        ),
        out_specs=(P(None, "lat", "lon"), P(None, None, None, ("lat", "lon"))),
        check_vma=False,
    )
```

profile of v0, /device:TPU:0, one launch (start us, length us, event | category | flops | bytes accessed | tf_op | source)
XLA Modules:
  0.0 14.6 jit_solution(2808029269496973377)
XLA Ops:
  0.6 12.7 %heat_transport.1 = (f32[4,64,128]{2,1,0:T(8,128)S(1)}, f32[4,4,8,10]{3,2,1,0:T(8,128)S(1)}) custom-call(f32[40,64,128]{2,1,0:T(8,128)} %bitcast.4, f32[40,64,128]{2,1,0:T(8,128)} %bitcast.5, s32[64,128]{1,0:T(8,128)} %flag_hbm.1, s32[64,128]{1,0:T(8,128)} %floor_hbm.1, s32[64,128]{1,0:T(8,128)} %label_hbm.1), custom_call_target="tpu_custom_call" | custom-call | tf_op jit(solution)/shard_map/heat_transport/pallas_call | solution.py:351
  13.3 0.7 %copy.9 = f32[4,64,128]{2,1,0:T(8,128)} copy(f32[4,64,128]{2,1,0:T(8,128)S(1)} %get-tuple-element.6) | data formatting | bytes 262144
  14.0 0.6 %copy.10 = f32[4,10,4,8]{1,3,2,0:T(8,128)} copy(f32[4,10,4,8]{1,3,2,0:T(8,128)S(1)} %bitcast.3) | data formatting | bytes 10240
where the time goes:
time: 14.8 us; the launch traced here: 14.6 us
  Pallas kernels  12.7 us (86%)
  local copies, waits for them, and re-layouts  1.29 us (9%)
  between operations  0.64 us (4%)
    pallas_call x1, Pallas kernels, shards(): pl.pallas_call(functools.partial(kernel, lat_devices, lon_devices, snapsh...  12.7 us
    unnamed x2, local copies, waits for them, and re-layouts  1.29 us

commit v1 on v0

v1 whole, which is shorter than its diff:
```python
import functools
import math

import jax
import jax.numpy as jnp
from jax import lax
from jax.experimental import pallas as pl
from jax.experimental.pallas import tpu as pltpu
from jax.sharding import PartitionSpec as P

BASINS = 10
MESH = pl.DeviceIdType.MESH
SUB = 8
LANES = 128
GROUPS = 2


def kernel(
    lat_devices, lon_devices, snapshots, levels, share_rows,
    flow_hbm, warmth_hbm, flag_hbm, floor_hbm, label_hbm,
    eddy_ref, transport_ref,
    columns, depth, flow, warmth, average, dots,
    halo_out, halo_in, stats, pair_stats, chip_stats, received, chip_sums, peer_sums, all_sums,
    edge_sums, peer_edge, edge_stats, peer_edge_stats, edge_total, edge_stats_total,
    load_first, load_columns, load_rest, halo_send, halo_recv,
    pair_send, pair_recv, stat_send, stat_recv, sum_send, sum_recv, share_send, share_recv,
    edge_send, edge_recv, edge_stat_send, edge_stat_recv,
):
    rows = flow.shape[1]
    blocks = rows // SUB
    last = blocks - 1
    half_blocks = blocks // GROUPS
    label_ref = columns.at[2]
    owners = SUB // share_rows
    planes = snapshots * levels
    parities, slots, packed = stats.shape[:3]
    group_slots = slots // GROUPS
    fields = dots.shape[1] // SUB
    used = BASINS * SUB
    chips = lon_devices // 2
    lat = lax.axis_index("lat")
    me = lax.axis_index("lon")
    core = lax.rem(me, 2)
    chip = me // 2
    mine = core if parities == 2 else 0
    theirs = 1 - core if parities == 2 else 0
    partner = (lat, me + 1 - 2 * core)
    own_slot = me // (owners * parities)
    scaling = 1.0 / math.sqrt(LANES * lon_devices)
    has_next = lat < lat_devices - 1

    def window(b):
        return pl.ds(b * SUB, SUB)

    def flow_copy(b):
        at = window(b)
        return pltpu.make_async_copy(flow_hbm.at[:, at, :], flow.at[:, at, :], load_rest.at[b // half_blocks])

    def warmth_copy(b):
        at = window(b)
        sem = load_first if b == 0 else load_rest.at[(b - 1) // half_blocks]
        return pltpu.make_async_copy(warmth_hbm.at[:, at, :], warmth.at[:, at, :], sem)

    def await_bytes(ref, sem):
        pltpu.make_async_copy(ref, ref, sem).wait()

    warmth_copy(0).start()
    for n, column in enumerate((flag_hbm, floor_hbm, label_hbm)):
        pltpu.make_async_copy(column, columns.at[n], load_columns).start()
    for g in range(GROUPS):
        for b in range(g * half_blocks, (g + 1) * half_blocks):
            flow_copy(b).start()
            if b < last:
                warmth_copy(b + 1).start()

    barrier = pltpu.get_barrier_semaphore()

    def greet(d, carry):
        pl.semaphore_signal(
            barrier, inc=1, device_id=(lat, lax.rem(me + d, lon_devices)), device_id_type=MESH
        )
        return carry

    @pl.when(has_next)
    def _():
        pl.semaphore_signal(barrier, inc=1, device_id=(lat + 1, me), device_id_type=MESH)

    lax.fori_loop(1, lon_devices, greet, 0)

    halo_copy = pltpu.make_async_remote_copy(
        src_ref=halo_out, dst_ref=halo_in, send_sem=halo_send, recv_sem=halo_recv,
        device_id=(jnp.maximum(lat - 1, 0), me), device_id_type=MESH,
    )

    def group(g):
        return pl.ds(g * group_slots, group_slots)

    def pair_copy(g):
        return pltpu.make_async_remote_copy(
            src_ref=stats.at[theirs, group(g)], dst_ref=pair_stats.at[group(g)],
            send_sem=pair_send, recv_sem=pair_recv.at[g],
            device_id=partner, device_id_type=MESH,
        )

    def sum_copy(g, to, source):
        return pltpu.make_async_remote_copy(
            src_ref=chip_sums.at[group(g)], dst_ref=peer_sums.at[source, group(g)],
            send_sem=sum_send, recv_sem=sum_recv,
            device_id=(lat, 2 * to + core), device_id_type=MESH,
        )

    def stat_slot(to):
        return (2 * to + core) // (owners * parities)

    def stat_copy(to, source):
        return pltpu.make_async_remote_copy(
            src_ref=chip_stats.at[stat_slot(to)], dst_ref=received.at[source],
            send_sem=stat_send, recv_sem=stat_recv,
            device_id=(lat, 2 * to + core), device_id_type=MESH,
        )

    share_copy = pltpu.make_async_remote_copy(
        src_ref=all_sums.at[mine], dst_ref=all_sums.at[mine],
        send_sem=share_send, recv_sem=share_recv, device_id=partner, device_id_type=MESH,
    )

    def edge_copy(to, source):
        return pltpu.make_async_remote_copy(
            src_ref=edge_sums, dst_ref=peer_edge.at[source],
            send_sem=edge_send, recv_sem=edge_recv,
            device_id=(lat, to), device_id_type=MESH,
        )

    def edge_stat_copy(source):
        return pltpu.make_async_remote_copy(
            src_ref=edge_stats, dst_ref=peer_edge_stats.at[source],
            send_sem=edge_stat_send, recv_sem=edge_stat_recv,
            device_id=(lat, lon_devices - 1), device_id_type=MESH,
        )

    def each_chip(action):
        def step(d, carry):
            action(lax.rem(chip + d, chips))
            return carry

        lax.fori_loop(1, chips, step, 0)

    def each_peer(action):
        def step(d, carry):
            action(lax.rem(me + d, lon_devices))
            return carry

        lax.fori_loop(1, lon_devices, step, 0)

    sub = lax.broadcasted_iota(jnp.int32, (SUB, LANES), 0)
    level = lax.broadcasted_iota(jnp.int32, (levels, SUB, LANES), 0).astype(jnp.float32)

    def next_row(here, after):
        first = lax.broadcasted_iota(jnp.int32, here.shape, here.ndim - 2) == 0
        return pltpu.roll(jnp.where(first, after, here), SUB - 1, here.ndim - 2)

    def both_halves(x):
        return x + pltpu.roll(x, levels, 0)

    def wet_cells(b):
        here = depth[window(b), :]
        limit = jnp.minimum(here, next_row(here, depth[window(b + 1), :]))
        return (level < limit[None]).astype(jnp.float32)

    def split_dot(values, member, out_rows):
        high = values.astype(jnp.bfloat16)
        low = (values - high.astype(jnp.float32)).astype(jnp.bfloat16)
        return lax.dot_general(
            jnp.concatenate([high, low], axis=1), jnp.concatenate([member, member], axis=1),
            (((1,), (1,)), ((), ())), preferred_element_type=jnp.float32,
        )

    def block_stats(b):
        at = window(b)
        wet = wet_cells(b)
        velocity = flow[:, at, :].reshape(snapshots, levels, SUB, LANES)
        here = warmth[:, at, :]
        point = (0.5 * (here + next_row(here, warmth[:, window(b + 1), :]))).reshape(
            snapshots, levels, SUB, LANES
        )
        mean_velocity = jnp.sum(velocity, axis=0) * (1.0 / snapshots)
        mean_warmth = jnp.sum(point, axis=0) * (1.0 / snapshots)
        cross = jnp.sum((velocity - mean_velocity) * (point - mean_warmth), axis=0) * (1.0 / snapshots)
        average[:, at, :] = mean_warmth
        values = jnp.concatenate(
            [
                (point * wet[None]).reshape(planes, SUB, LANES),
                wet,
                wet,
                (velocity * wet[None]).reshape(planes, SUB, LANES),
                mean_velocity * mean_warmth * wet,
                cross * wet,
            ],
            axis=0,
        ).reshape(-1, LANES)
        labels = label_ref[at, :]
        member = jnp.concatenate(
            [(labels == n).astype(jnp.float32) for n in range(LANES // SUB)], axis=0
        ).astype(jnp.bfloat16)
        dots[b] = split_dot(values, member, fields * SUB)
        row_of = lax.rem(lax.broadcasted_iota(jnp.int32, (fields, LANES), 1), SUB)
        zonal = dots[b, pl.ds(0, fields, stride=SUB), :]
        for j in range(1, SUB):
            zonal = jnp.where(row_of == j, dots[b, pl.ds(j, fields, stride=SUB), :], zonal)
        half = packed // 2
        rest = zonal[packed:]
        spare = lax.broadcasted_iota(jnp.int32, (half, LANES), 1) >= used
        stats[b % parities, b // parities] = jnp.concatenate(
            [
                jnp.where(spare, pltpu.roll(rest, used, 1), zonal[:half]),
                jnp.where(spare, pltpu.roll(rest, 2 * used - LANES, 1), zonal[half:packed]),
            ],
            axis=0,
        )

    def sums_of(zonal):
        warmth_sum = both_halves(jnp.sum(zonal[:planes].reshape(planes // SUB, SUB, LANES), axis=0))
        return jnp.where(sub < levels, warmth_sum, zonal[planes : planes + SUB])

    def pair_sums(g):
        pair_copy(g).wait_recv()
        for s in range(g * group_slots, (g + 1) * group_slots):
            total = stats[mine, s] + pair_stats[s]
            chip_stats[s] = total
            chip_sums[s] = sums_of(total)

    def send_group(g):
        each_chip(lambda to: sum_copy(g, to, chip).start())

        def send_stats(to):
            @pl.when(stat_slot(to) // group_slots == g)
            def _():
                stat_copy(to, chip).start()

        each_chip(send_stats)

    warmth_copy(0).wait()
    await_bytes(columns, load_columns)
    depth[pl.ds(0, rows), :] = (columns[0] * columns[1]).astype(jnp.float32)
    depth[pl.ds(rows, SUB), :] = jnp.zeros((SUB, LANES), jnp.float32)
    warmth[:, rows, :] = jnp.zeros((planes, LANES), jnp.float32)
    halo_out[pl.ds(0, planes), :] = warmth[:, 0, :]
    halo_out[pl.ds(planes, SUB), :] = depth[pl.ds(0, SUB), :]

    pl.semaphore_wait(barrier, lon_devices - 1 + (lat > 0).astype(jnp.int32))

    @pl.when(lat > 0)
    def _():
        halo_copy.start()

    def load_group(g):
        count = half_blocks * SUB
        await_bytes(flow.at[:, pl.ds(g * count, count), :], load_rest.at[g])
        count = (half_blocks if g < GROUPS - 1 else half_blocks - 1) * SUB
        await_bytes(warmth.at[:, pl.ds(0, count), :], load_rest.at[g])

    load_group(0)
    for b in range(half_blocks):
        block_stats(b)
    pair_copy(0).start()
    load_group(1)
    for b in range(half_blocks, blocks):
        block_stats(b)
    pair_copy(1).start()
    pair_sums(0)
    send_group(0)
    pair_sums(1)
    send_group(1)

    lanes = lax.broadcasted_iota(jnp.int32, (SUB, LANES), 1)
    edge_total[...] = jnp.zeros((SUB, LANES), jnp.float32)
    edge_stats_total[...] = jnp.zeros((2 * SUB, LANES), jnp.float32)

    @pl.when(has_next)
    def _():
        at = rows - 1
        members = lax.broadcasted_iota(jnp.int32, (LANES, LANES), 0)
        chosen = jnp.logical_and(
            lax.rem(members, SUB) == SUB - 1, label_ref[pl.ds(at, 1), :] == members // SUB
        )
        member = chosen.astype(jnp.float32).astype(jnp.bfloat16)
        velocity = flow[:, at, :].reshape(planes // SUB, SUB, LANES)
        mean_velocity = both_halves(jnp.sum(velocity, axis=0)) * (1.0 / snapshots)
        here = warmth[:, at, :]
        halo_copy.wait_recv()
        limit = jnp.minimum(depth[pl.ds(at, 1), :], halo_in[pl.ds(planes, 1), :])
        wet = (lax.rem(sub, levels).astype(jnp.float32) < limit).astype(jnp.float32)
        point = (0.5 * (here + halo_in[pl.ds(0, planes), :])).reshape(planes // SUB, SUB, LANES)
        mean_warmth = both_halves(jnp.sum(point, axis=0)) * (1.0 / snapshots)
        cross = both_halves(
            jnp.sum((velocity - mean_velocity) * (point - mean_warmth), axis=0)
        ) * (1.0 / snapshots)
        average[:, at, :] = mean_warmth[:levels]
        depth[pl.ds(rows, SUB), :] = halo_in[pl.ds(planes, SUB), :]
        values = jnp.concatenate(
            [
                (point * wet).reshape(planes, LANES),
                wet,
                (velocity * wet).reshape(planes, LANES),
                jnp.where(sub < levels, mean_velocity * mean_warmth, cross) * wet,
            ],
            axis=0,
        )
        zonal = split_dot(values, member, fields)
        edge_sums[...] = sums_of(zonal)
        each_peer(lambda to: edge_copy(to, me).start())
        parts = [zonal[SUB * n : SUB * (n + 1)] for n in range(fields // SUB)]
        first = parts[0]
        for n in range(1, SUB):
            first = first + pltpu.roll(parts[n], LANES - n, 1)
        second = parts[SUB]
        for n in range(SUB + 1, fields // SUB):
            second = second + pltpu.roll(parts[n], LANES - (n - SUB), 1)
        edge_stats[...] = jnp.concatenate([first, second], axis=0)

        @pl.when(me < lon_devices - 1)
        def _():
            edge_stat_copy(me).start()

    def block_eddy(b, block_sums):
        at = pl.ds(b * SUB, SUB)
        wet = wet_cells(b)
        index = label_ref[at, :] * SUB + sub
        bar = block_sums / jnp.maximum(pltpu.roll(block_sums, levels, 0), 1.0) * (1.0 / snapshots)
        for k in range(levels):
            cells = jnp.take_along_axis(
                jnp.broadcast_to(bar[k : k + 1], (SUB, LANES)), index, axis=1
            )
            eddy_ref[k, at, :] = wet[k] * (average[k, at, :] - cells)

    def add_sums(d, total):
        source = lax.rem(chip + chips - d, chips)
        return total + peer_sums[pl.ds(source, 1)][0]

    await_bytes(peer_sums.at[pl.ds(0, chips - 1)], sum_recv)
    all_sums[mine] = lax.fori_loop(1, chips, add_sums, chip_sums[...], unroll=chips <= SUB)
    if parities == 2:
        share_copy.start()

    def add_received(d, total):
        source = lax.rem(chip + chips - d, chips)
        return total + received[pl.ds(source, 1)][0]

    await_bytes(received.at[pl.ds(0, chips - 1)], stat_recv)
    total = lax.fori_loop(
        1, chips, add_received, chip_stats[pl.ds(own_slot, 1)][0], unroll=chips <= SUB
    )
    if parities == 2:
        share_copy.wait_recv()
    for b in range(last):
        block_eddy(b, all_sums[b % parities, b // parities])

    @pl.when(has_next)
    def _():
        def add_edge(d, total):
            source = lax.rem(me + lon_devices - d, lon_devices)
            return total + peer_edge[pl.ds(source, 1)][0]

        await_bytes(peer_edge.at[pl.ds(0, lon_devices - 1)], edge_recv)
        edge_total[...] = lax.fori_loop(
            1, lon_devices, add_edge, edge_sums[...], unroll=lon_devices <= SUB
        )

        @pl.when(me == lon_devices - 1)
        def _():
            def add_edge_stats(d, total):
                source = lax.rem(me + lon_devices - d, lon_devices)
                return total + peer_edge_stats[pl.ds(source, 1)][0]

            await_bytes(peer_edge_stats.at[pl.ds(0, lon_devices - 1)], edge_stat_recv)
            edge_stats_total[...] = lax.fori_loop(
                1, lon_devices, add_edge_stats, edge_stats[...], unroll=lon_devices <= SUB
            )

    block_eddy(last, all_sums[last % parities, last // parities] + edge_total[...])
    half = packed // 2
    lane = lax.broadcasted_iota(jnp.int32, (half, LANES), 1)
    total = jnp.concatenate(
        [
            total,
            jnp.where(
                lane < LANES - used,
                pltpu.roll(total[:half], LANES - used, 1),
                pltpu.roll(total[half:], 2 * LANES - 2 * used, 1),
            ),
        ],
        axis=0,
    )
    extra = edge_stats_total[...]
    edge_lane = lax.rem(lanes, SUB) == SUB - 1
    pieces = []
    for n in range(fields // SUB):
        part = extra[:SUB] if n < SUB else extra[SUB:]
        if n % SUB:
            part = pltpu.roll(part, n % SUB, 1)
        pieces.append(total[SUB * n : SUB * (n + 1)] + jnp.where(edge_lane, part, 0.0))
    shape = (planes // SUB, SUB, LANES)
    per = planes // SUB
    count = pieces[per]
    divisor = jnp.maximum(count, 1.0)
    means_t = jnp.stack(pieces[:per]) / divisor
    means_v = jnp.stack(pieces[per + 1 : 2 * per + 1]) / divisor
    bar_v = both_halves(jnp.sum(means_v, axis=0)) * (1.0 / snapshots)
    bar_t = both_halves(jnp.sum(means_t, axis=0)) * (1.0 / snapshots)
    swing = both_halves(jnp.sum((means_v - bar_v) * (means_t - bar_t), axis=0)) * (1.0 / snapshots)
    upper = jnp.where(sub < levels, scaling * count * bar_v * bar_t, scaling * count * swing)
    lower = scaling * pieces[2 * per + 1] - upper
    if owners > 1:
        shift = LANES - lax.rem(me, owners) * share_rows
        upper = pltpu.roll(upper, shift, 1)
        lower = pltpu.roll(lower, shift, 1)
    spread = lax.rem(lanes * SUB + sub, LANES)
    for c, part in enumerate((upper, lower, upper, lower)):
        for k in range(levels):
            row = c // 2 * levels + k
            table = jnp.take_along_axis(
                jnp.broadcast_to(part[row : row + 1], (SUB, LANES)), spread, axis=1
            )
            transport_ref[c, k] = table[:share_rows, :BASINS]

    @pl.when(lat > 0)
    def _():
        halo_copy.wait_send()

    await_bytes(pair_stats, pair_send)
    await_bytes(peer_sums.at[pl.ds(0, chips - 1)], sum_send)
    await_bytes(received.at[pl.ds(0, chips - 1)], stat_send)
    if parities == 2:
        share_copy.wait_send()

    @pl.when(has_next)
    def _():
        await_bytes(peer_edge.at[pl.ds(0, lon_devices - 1)], edge_send)

        @pl.when(me < lon_devices - 1)
        def _():
            edge_stat_copy(me).wait_send()


def store(eddy_ref, transport_ref, eddy_hbm, transport_hbm, sems):
    copies = (
        pltpu.make_async_copy(eddy_ref, eddy_hbm, sems.at[0]),
        pltpu.make_async_copy(transport_ref, transport_hbm, sems.at[1]),
    )
    for copy in copies:
        copy.start()
    for copy in copies:
        copy.wait()


def shards(
    lat_devices, lon_devices,
    poleward_flow, potential_warmth, water_profile_flag, floor_count, catchment_label_for_site,
):
    snapshots, levels, rows, columns = poleward_flow.shape
    share_rows = rows // lon_devices
    blocks = rows // SUB
    planes = snapshots * levels
    fields = 2 * planes + 4 * levels
    packed = fields * 2 // 3
    chips = lon_devices // 2
    parities = 2 if share_rows == SUB else 1
    slots = blocks // parities
    f32, i32, vmem, dma = jnp.float32, jnp.int32, pltpu.VMEM, pltpu.SemaphoreType.DMA
    eddy_shape = (levels, rows, columns)
    transport_shape = (4, levels, share_rows, BASINS)
    eddy_temp, transport = pl.pallas_call(
        functools.partial(kernel, lat_devices, lon_devices, snapshots, levels, share_rows),
        out_shape=(vmem(eddy_shape, f32), vmem(transport_shape, f32)),
        in_specs=[pl.BlockSpec(memory_space=pltpu.HBM)] * 5,
        out_specs=(pl.BlockSpec(memory_space=vmem), pl.BlockSpec(memory_space=vmem)),
        scratch_shapes=[
            vmem((3, rows, columns), i32),
            vmem((rows + SUB, columns), f32),
            vmem((planes, rows, columns), f32),
            vmem((planes, rows + SUB, columns), f32),
            vmem((levels, rows, columns), f32),
            vmem((blocks, fields * SUB, LANES), f32),
            vmem((planes + SUB, LANES), f32),
            vmem((planes + SUB, LANES), f32),
            vmem((parities, slots, packed, LANES), f32),
            vmem((slots, packed, LANES), f32),
            vmem((slots, packed, LANES), f32),
            vmem((chips, packed, LANES), f32),
            vmem((slots, SUB, LANES), f32),
            vmem((chips, slots, SUB, LANES), f32),
            vmem((parities, slots, SUB, LANES), f32),
            vmem((SUB, LANES), f32),
            vmem((lon_devices, SUB, LANES), f32),
            vmem((2 * SUB, LANES), f32),
            vmem((lon_devices, 2 * SUB, LANES), f32),
            vmem((SUB, LANES), f32),
            vmem((2 * SUB, LANES), f32),
            dma,
            dma,
            dma((GROUPS,)),
            dma,
            dma,
            dma,
            dma((GROUPS,)),
            dma,
            dma,
            dma,
            dma,
            dma,
            dma,
            dma,
            dma,
            dma,
            dma,
        ],
        compiler_params=pltpu.CompilerParams(
            collective_id=0, has_side_effects=True, vmem_limit_bytes=62 * 1024 * 1024
        ),
        name="heat_transport",
    )(
        poleward_flow.reshape(planes, rows, columns),
        potential_warmth.reshape(planes, rows, columns),
        water_profile_flag,
        floor_count,
        catchment_label_for_site,
    )
    eddy_temp, transport = pl.pallas_call(
        store,
        out_shape=(
            jax.ShapeDtypeStruct(eddy_shape, f32), jax.ShapeDtypeStruct(transport_shape, f32)
        ),
        in_specs=[pl.BlockSpec(memory_space=vmem)] * 2,
        out_specs=(pl.BlockSpec(memory_space=pltpu.HBM), pl.BlockSpec(memory_space=pltpu.HBM)),
        scratch_shapes=[dma((2,))],
        name="store_results",
    )(
        pltpu.with_memory_space_constraint(eddy_temp, vmem),
        pltpu.with_memory_space_constraint(transport, vmem),
    )
    return eddy_temp, jnp.transpose(transport, (0, 3, 1, 2))


def solution(mesh):
    return jax.shard_map(
        functools.partial(shards, mesh.shape["lat"], mesh.shape["lon"]),
        mesh=mesh,
        in_specs=(
            P(None, None, "lat", "lon"),
            P(None, None, "lat", "lon"),
            P("lat", "lon"),
            P("lat", "lon"),
            P("lat", "lon"),
        ),
        out_specs=(P(None, "lat", "lon"), P(None, None, None, ("lat", "lon"))),
        check_vma=False,
    )
```

time: 14.8 us -> 12.8 us (0.86)
  local copies, waits for them, and re-layouts: 1.29 us -> 0 us
  Pallas kernels: 12.7 us -> 12 us
    pallas_call x1, Pallas kernels: 12.7 us -> 11.3 us  [shards(): pl.pallas_call(functools.partial(kernel, lat_devices, lon_devices, snapsh...]
    unnamed x2 -> x0, local copies, waits for them, and re-layouts: 1.29 us -> none
    pallas_call x0 -> x1, Pallas kernels: none -> 0.69 us  [shards(): pl.pallas_call(store, out_shape=(jax.ShapeDtypeStruct(eddy_shape, f32), j...]
where the time goes in v1:
time: 12.8 us; the launch traced here: 12.6 us
  Pallas kernels  12 us (94%)
  between operations  0.64 us (5%)
    pallas_call x1, Pallas kernels, shards(): pl.pallas_call(functools.partial(kernel, lat_devices, lon_devices, snapsh...  11.3 us
    pallas_call x1, Pallas kernels, shards(): pl.pallas_call(store, out_shape=(jax.ShapeDtypeStruct(eddy_shape, f32), j...  0.69 us

profile of v1, /device:TPU:0, one launch (start us, length us, event | category | flops | bytes accessed | tf_op | source)
XLA Modules:
  0.0 12.6 jit_solution(3541176713204842712)
XLA Ops:
  0.6 11.3 %heat_transport.1 = (f32[4,64,128]{2,1,0:T(8,128)S(1)}, f32[4,4,8,10]{3,2,1,0:T(8,128)S(1)}) custom-call(f32[40,64,128]{2,1,0:T(8,128)} %bitcast.3, f32[40,64,128]{2,1,0:T(8,128)} %bitcast.4, s32[64,128]{1,0:T(8,128)} %flag_hbm.1, s32[64,128]{1,0:T(8,128)} %floor_hbm.1, s32[64,128]{1,0:T(8,128)} %label_hbm.1), custom_call_target="tpu_custom_call" | custom-call | tf_op jit(solution)/shard_map/heat_transport/pallas_call | solution.py:472
  11.9 0.7 %store_results.1 = (f32[4,64,128]{2,1,0:T(8,128)}, f32[4,4,8,10]{3,2,1,0:T(8,128)}) custom-call(f32[4,64,128]{2,1,0:T(8,128)S(1)} %get-tuple-element.6.eddy_ref, f32[4,4,8,10]{3,2,1,0:T(8,128)S(1)} %get-tuple-element.7.transport_ref), custom_call_target="tpu_custom_call" | custom-call | tf_op jit(solution)/shard_map/store_results/pallas_call | solution.py:528

commit v2 on v1

--- a/solution.py
+++ b/solution.py
@@ -19,11 +19,11 @@
     lat_devices, lon_devices, snapshots, levels, share_rows,
     flow_hbm, warmth_hbm, flag_hbm, floor_hbm, label_hbm,
     eddy_ref, transport_ref,
-    columns, depth, flow, warmth, average, dots,
-    halo_out, halo_in, stats, pair_stats, chip_stats, received, chip_sums, peer_sums, all_sums,
+    columns, depth, flow, warmth, average, dots, mean_dots, members,
+    halo_out, halo_in, stats, pair_stats, chip_stats, received, sums, pair_sums, chip_sums, peer_sums, all_sums,
     edge_sums, peer_edge, edge_stats, peer_edge_stats, edge_total, edge_stats_total,
-    load_first, load_columns, load_rest, halo_send, halo_recv,
-    pair_send, pair_recv, stat_send, stat_recv, sum_send, sum_recv, share_send, share_recv,
+    load_first, load_warmth, load_flow, halo_send, halo_recv,
+    sums_pair_send, sums_pair_recv, pair_send, pair_recv, stat_send, stat_recv, sum_send, sum_recv, share_send, share_recv,
     edge_send, edge_recv, edge_stat_send, edge_stat_recv,
 ):
     rows = flow.shape[1]
@@ -54,24 +54,27 @@
 
     def flow_copy(b):
         at = window(b)
-        return pltpu.make_async_copy(flow_hbm.at[:, at, :], flow.at[:, at, :], load_rest.at[b // half_blocks])
+        return pltpu.make_async_copy(
+            flow_hbm.at[:, at, :], flow.at[:, at, :], load_flow.at[b // half_blocks]
+        )
 
     def warmth_copy(b):
         at = window(b)
-        sem = load_first if b == 0 else load_rest.at[(b - 1) // half_blocks]
+        sem = load_warmth if b else load_first
         return pltpu.make_async_copy(warmth_hbm.at[:, at, :], warmth.at[:, at, :], sem)
 
     def await_bytes(ref, sem):
         pltpu.make_async_copy(ref, ref, sem).wait()
 
-    warmth_copy(0).start()
+    def await_flow(g):
+        await_bytes(flow.at[:, pl.ds(0, half_blocks * SUB), :], load_flow.at[g])
+
     for n, column in enumerate((flag_hbm, floor_hbm, label_hbm)):
-        pltpu.make_async_copy(column, columns.at[n], load_columns).start()
-    for g in range(GROUPS):
-        for b in range(g * half_blocks, (g + 1) * half_blocks):
-            flow_copy(b).start()
-            if b < last:
-                warmth_copy(b + 1).start()
+        pltpu.make_async_copy(column, columns.at[n], load_first).start()
+    for b in range(blocks):
+        warmth_copy(b).start()
+    for b in range(blocks):
+        flow_copy(b).start()
 
     barrier = pltpu.get_barrier_semaphore()
 
@@ -102,9 +105,14 @@
             device_id=partner, device_id_type=MESH,
         )
 
-    def sum_copy(g, to, source):
+    sums_pair_copy = pltpu.make_async_remote_copy(
+        src_ref=sums.at[theirs], dst_ref=pair_sums,
+        send_sem=sums_pair_send, recv_sem=sums_pair_recv, device_id=partner, device_id_type=MESH,
+    )
+
+    def sum_copy(to, source):
         return pltpu.make_async_remote_copy(
-            src_ref=chip_sums.at[group(g)], dst_ref=peer_sums.at[source, group(g)],
+            src_ref=chip_sums, dst_ref=peer_sums.at[source],
             send_sem=sum_send, recv_sem=sum_recv,
             device_id=(lat, 2 * to + core), device_id_type=MESH,
         )
@@ -167,13 +175,38 @@
         limit = jnp.minimum(here, next_row(here, depth[window(b + 1), :]))
         return (level < limit[None]).astype(jnp.float32)
 
-    def split_dot(values, member, out_rows):
+    def split_dot(values, member):
         high = values.astype(jnp.bfloat16)
         low = (values - high.astype(jnp.float32)).astype(jnp.bfloat16)
         return lax.dot_general(
             jnp.concatenate([high, low], axis=1), jnp.concatenate([member, member], axis=1),
             (((1,), (1,)), ((), ())), preferred_element_type=jnp.float32,
         )
+
+    def by_row(ref, count):
+        row_of = lax.rem(lax.broadcasted_iota(jnp.int32, (count, LANES), 1), SUB)
+        zonal = ref[pl.ds(0, count, stride=SUB), :]
+        for j in range(1, SUB):
+            zonal = jnp.where(row_of == j, ref[pl.ds(j, count, stride=SUB), :], zonal)
+        return zonal
+
+    def block_means(b):
+        at = window(b)
+        wet = wet_cells(b)
+        here = jnp.sum(warmth[:, at, :].reshape(snapshots, levels, SUB, LANES), axis=0)
+        after = jnp.sum(
+            warmth[:, window(b + 1), :].reshape(snapshots, levels, SUB, LANES)[:, :, :1], axis=0
+        )
+        mean_warmth = (here + next_row(here, after)) * (0.5 / snapshots)
+        average[:, at, :] = mean_warmth
+        labels = label_ref[at, :]
+        member = jnp.concatenate(
+            [(labels == n).astype(jnp.float32) for n in range(LANES // SUB)], axis=0
+        ).astype(jnp.bfloat16)
+        members[b] = member
+        values = jnp.concatenate([mean_warmth * wet, wet], axis=0).reshape(-1, LANES)
+        mean_dots[b] = split_dot(values, member)
+        sums[b % parities, b // parities] = by_row(mean_dots.at[b], 2 * levels)
 
     def block_stats(b):
         at = window(b)
@@ -183,10 +216,9 @@
         point = (0.5 * (here + next_row(here, warmth[:, window(b + 1), :]))).reshape(
             snapshots, levels, SUB, LANES
         )
+        mean_warmth = average[:, at, :]
         mean_velocity = jnp.sum(velocity, axis=0) * (1.0 / snapshots)
-        mean_warmth = jnp.sum(point, axis=0) * (1.0 / snapshots)
         cross = jnp.sum((velocity - mean_velocity) * (point - mean_warmth), axis=0) * (1.0 / snapshots)
-        average[:, at, :] = mean_warmth
         values = jnp.concatenate(
             [
                 (point * wet[None]).reshape(planes, SUB, LANES),
@@ -198,15 +230,8 @@
             ],
             axis=0,
         ).reshape(-1, LANES)
-        labels = label_ref[at, :]
-        member = jnp.concatenate(
-            [(labels == n).astype(jnp.float32) for n in range(LANES // SUB)], axis=0
-        ).astype(jnp.bfloat16)
-        dots[b] = split_dot(values, member, fields * SUB)
-        row_of = lax.rem(lax.broadcasted_iota(jnp.int32, (fields, LANES), 1), SUB)
-        zonal = dots[b, pl.ds(0, fields, stride=SUB), :]
-        for j in range(1, SUB):
-            zonal = jnp.where(row_of == j, dots[b, pl.ds(j, fields, stride=SUB), :], zonal)
+        dots[b] = split_dot(values, members[b])
+        zonal = by_row(dots.at[b], fields)
         half = packed // 2
         rest = zonal[packed:]
         spare = lax.broadcasted_iota(jnp.int32, (half, LANES), 1) >= used
@@ -220,18 +245,19 @@
 
     def sums_of(zonal):
         warmth_sum = both_halves(jnp.sum(zonal[:planes].reshape(planes // SUB, SUB, LANES), axis=0))
-        return jnp.where(sub < levels, warmth_sum, zonal[planes : planes + SUB])
-
-    def pair_sums(g):
+        return jnp.where(sub < levels, warmth_sum * (1.0 / snapshots), zonal[planes : planes + SUB])
+
+    def add_pair(g):
         pair_copy(g).wait_recv()
         for s in range(g * group_slots, (g + 1) * group_slots):
-            total = stats[mine, s] + pair_stats[s]
-            chip_stats[s] = total
-            chip_sums[s] = sums_of(total)
-
-    def send_group(g):
-        each_chip(lambda to: sum_copy(g, to, chip).start())
-
+            chip_stats[s] = stats[mine, s] + pair_stats[s]
+
+    def send_sums():
+        sums_pair_copy.wait_recv()
+        chip_sums[...] = sums[mine] + pair_sums[...]
+        each_chip(lambda to: sum_copy(to, chip).start())
+
+    def send_group_stats(g):
         def send_stats(to):
             @pl.when(stat_slot(to) // group_slots == g)
             def _():
@@ -239,8 +265,8 @@
 
         each_chip(send_stats)
 
-    warmth_copy(0).wait()
-    await_bytes(columns, load_columns)
+    await_bytes(columns, load_first)
+    await_bytes(warmth.at[:, window(0), :], load_first)
     depth[pl.ds(0, rows), :] = (columns[0] * columns[1]).astype(jnp.float32)
     depth[pl.ds(rows, SUB), :] = jnp.zeros((SUB, LANES), jnp.float32)
     warmth[:, rows, :] = jnp.zeros((planes, LANES), jnp.float32)
@@ -253,35 +279,39 @@
     def _():
         halo_copy.start()
 
-    def load_group(g):
-        count = half_blocks * SUB
-        await_bytes(flow.at[:, pl.ds(g * count, count), :], load_rest.at[g])
-        count = (half_blocks if g < GROUPS - 1 else half_blocks - 1) * SUB
-        await_bytes(warmth.at[:, pl.ds(0, count), :], load_rest.at[g])
-
-    load_group(0)
+    await_bytes(warmth.at[:, pl.ds(0, last * SUB), :], load_warmth)
+    for b in range(blocks):
+        block_means(b)
+    sums_pair_copy.start()
+    await_flow(0)
     for b in range(half_blocks):
         block_stats(b)
     pair_copy(0).start()
-    load_group(1)
+    @pl.when(core == 0)
+    def _():
+        send_sums()
+
+    await_flow(1)
     for b in range(half_blocks, blocks):
         block_stats(b)
     pair_copy(1).start()
-    pair_sums(0)
-    send_group(0)
-    pair_sums(1)
-    send_group(1)
+
+    @pl.when(core == 1)
+    def _():
+        send_sums()
+
+    add_pair(0)
+    send_group_stats(0)
 
     lanes = lax.broadcasted_iota(jnp.int32, (SUB, LANES), 1)
     edge_total[...] = jnp.zeros((SUB, LANES), jnp.float32)
-    edge_stats_total[...] = jnp.zeros((2 * SUB, LANES), jnp.float32)
 
     @pl.when(has_next)
     def _():
         at = rows - 1
-        members = lax.broadcasted_iota(jnp.int32, (LANES, LANES), 0)
+        column = lax.broadcasted_iota(jnp.int32, (LANES, LANES), 0)
         chosen = jnp.logical_and(
-            lax.rem(members, SUB) == SUB - 1, label_ref[pl.ds(at, 1), :] == members // SUB
+            lax.rem(column, SUB) == SUB - 1, label_ref[pl.ds(at, 1), :] == column // SUB
         )
         member = chosen.astype(jnp.float32).astype(jnp.bfloat16)
         velocity = flow[:, at, :].reshape(planes // SUB, SUB, LANES)
@@ -306,7 +336,7 @@
             ],
             axis=0,
         )
-        zonal = split_dot(values, member, fields)
+        zonal = split_dot(values, member)
         edge_sums[...] = sums_of(zonal)
         each_peer(lambda to: edge_copy(to, me).start())
         parts = [zonal[SUB * n : SUB * (n + 1)] for n in range(fields // SUB)]
@@ -322,11 +352,14 @@
         def _():
             edge_stat_copy(me).start()
 
+    add_pair(1)
+    send_group_stats(1)
+
     def block_eddy(b, block_sums):
         at = pl.ds(b * SUB, SUB)
         wet = wet_cells(b)
         index = label_ref[at, :] * SUB + sub
-        bar = block_sums / jnp.maximum(pltpu.roll(block_sums, levels, 0), 1.0) * (1.0 / snapshots)
+        bar = block_sums / jnp.maximum(pltpu.roll(block_sums, levels, 0), 1.0)
         for k in range(levels):
             cells = jnp.take_along_axis(
                 jnp.broadcast_to(bar[k : k + 1], (SUB, LANES)), index, axis=1
@@ -342,19 +375,74 @@
     if parities == 2:
         share_copy.start()
 
+    def write_transport(total, early):
+        half = packed // 2
+        lane = lax.broadcasted_iota(jnp.int32, (half, LANES), 1)
+        total = jnp.concatenate(
+            [
+                total,
+                jnp.where(
+                    lane < LANES - used,
+                    pltpu.roll(total[:half], LANES - used, 1),
+                    pltpu.roll(total[half:], 2 * LANES - 2 * used, 1),
+                ),
+            ],
+            axis=0,
+        )
+        extra = None if early else edge_stats_total[...]
+        edge_lane = lax.rem(lanes, SUB) == SUB - 1
+        pieces = []
+        for n in range(fields // SUB):
+            piece = total[SUB * n : SUB * (n + 1)]
+            if extra is not None:
+                part = extra[:SUB] if n < SUB else extra[SUB:]
+                if n % SUB:
+                    part = pltpu.roll(part, n % SUB, 1)
+                piece = piece + jnp.where(edge_lane, part, 0.0)
+            pieces.append(piece)
+        shape = (planes // SUB, SUB, LANES)
+        per = planes // SUB
+        count = pieces[per]
+        divisor = jnp.maximum(count, 1.0)
+        means_t = jnp.stack(pieces[:per]) / divisor
+        means_v = jnp.stack(pieces[per + 1 : 2 * per + 1]) / divisor
+        bar_v = both_halves(jnp.sum(means_v, axis=0)) * (1.0 / snapshots)
+        bar_t = both_halves(jnp.sum(means_t, axis=0)) * (1.0 / snapshots)
+        swing = both_halves(jnp.sum((means_v - bar_v) * (means_t - bar_t), axis=0)) * (1.0 / snapshots)
+        upper = jnp.where(sub < levels, scaling * count * bar_v * bar_t, scaling * count * swing)
+        lower = scaling * pieces[2 * per + 1] - upper
+        if owners > 1:
+            shift = LANES - lax.rem(me, owners) * share_rows
+            upper = pltpu.roll(upper, shift, 1)
+            lower = pltpu.roll(lower, shift, 1)
+        spread = lax.rem(lanes * SUB + sub, LANES)
+        for c, part in enumerate((upper, lower, upper, lower)):
+            for k in range(levels):
+                row = c // 2 * levels + k
+                table = jnp.take_along_axis(
+                    jnp.broadcast_to(part[row : row + 1], (SUB, LANES)), spread, axis=1
+                )
+                transport_ref[c, k] = table[:share_rows, :BASINS]
+
     def add_received(d, total):
         source = lax.rem(chip + chips - d, chips)
         return total + received[pl.ds(source, 1)][0]
 
-    await_bytes(received.at[pl.ds(0, chips - 1)], stat_recv)
-    total = lax.fori_loop(
-        1, chips, add_received, chip_stats[pl.ds(own_slot, 1)][0], unroll=chips <= SUB
-    )
     if parities == 2:
         share_copy.wait_recv()
     for b in range(last):
         block_eddy(b, all_sums[b % parities, b // parities])
 
+    await_bytes(received.at[pl.ds(0, chips - 1)], stat_recv)
+    total = lax.fori_loop(
+        1, chips, add_received, chip_stats[pl.ds(own_slot, 1)][0], unroll=chips <= SUB
+    )
+    late = jnp.logical_and(has_next, me == lon_devices - 1)
+
+    @pl.when(jnp.logical_not(late))
+    def _():
+        write_transport(total, True)
+
     @pl.when(has_next)
     def _():
         def add_edge(d, total):
@@ -366,67 +454,24 @@
             1, lon_devices, add_edge, edge_sums[...], unroll=lon_devices <= SUB
         )
 
-        @pl.when(me == lon_devices - 1)
-        def _():
-            def add_edge_stats(d, total):
-                source = lax.rem(me + lon_devices - d, lon_devices)
-                return total + peer_edge_stats[pl.ds(source, 1)][0]
-
-            await_bytes(peer_edge_stats.at[pl.ds(0, lon_devices - 1)], edge_stat_recv)
-            edge_stats_total[...] = lax.fori_loop(
-                1, lon_devices, add_edge_stats, edge_stats[...], unroll=lon_devices <= SUB
-            )
-
     block_eddy(last, all_sums[last % parities, last // parities] + edge_total[...])
-    half = packed // 2
-    lane = lax.broadcasted_iota(jnp.int32, (half, LANES), 1)
-    total = jnp.concatenate(
-        [
-            total,
-            jnp.where(
-                lane < LANES - used,
-                pltpu.roll(total[:half], LANES - used, 1),
-                pltpu.roll(total[half:], 2 * LANES - 2 * used, 1),
-            ),
-        ],
-        axis=0,
-    )
-    extra = edge_stats_total[...]
-    edge_lane = lax.rem(lanes, SUB) == SUB - 1
-    pieces = []
-    for n in range(fields // SUB):
-        part = extra[:SUB] if n < SUB else extra[SUB:]
-        if n % SUB:
-            part = pltpu.roll(part, n % SUB, 1)
-        pieces.append(total[SUB * n : SUB * (n + 1)] + jnp.where(edge_lane, part, 0.0))
-    shape = (planes // SUB, SUB, LANES)
-    per = planes // SUB
-    count = pieces[per]
-    divisor = jnp.maximum(count, 1.0)
-    means_t = jnp.stack(pieces[:per]) / divisor
-    means_v = jnp.stack(pieces[per + 1 : 2 * per + 1]) / divisor
-    bar_v = both_halves(jnp.sum(means_v, axis=0)) * (1.0 / snapshots)
-    bar_t = both_halves(jnp.sum(means_t, axis=0)) * (1.0 / snapshots)
-    swing = both_halves(jnp.sum((means_v - bar_v) * (means_t - bar_t), axis=0)) * (1.0 / snapshots)
-    upper = jnp.where(sub < levels, scaling * count * bar_v * bar_t, scaling * count * swing)
-    lower = scaling * pieces[2 * per + 1] - upper
-    if owners > 1:
-        shift = LANES - lax.rem(me, owners) * share_rows
-        upper = pltpu.roll(upper, shift, 1)
-        lower = pltpu.roll(lower, shift, 1)
-    spread = lax.rem(lanes * SUB + sub, LANES)
-    for c, part in enumerate((upper, lower, upper, lower)):
-        for k in range(levels):
-            row = c // 2 * levels + k
-            table = jnp.take_along_axis(
-                jnp.broadcast_to(part[row : row + 1], (SUB, LANES)), spread, axis=1
-            )
-            transport_ref[c, k] = table[:share_rows, :BASINS]
+    @pl.when(late)
+    def _():
+        def add_edge_stats(d, total):
+            source = lax.rem(me + lon_devices - d, lon_devices)
+            return total + peer_edge_stats[pl.ds(source, 1)][0]
+
+        await_bytes(peer_edge_stats.at[pl.ds(0, lon_devices - 1)], edge_stat_recv)
+        edge_stats_total[...] = lax.fori_loop(
+            1, lon_devices, add_edge_stats, edge_stats[...], unroll=lon_devices <= SUB
+        )
+        write_transport(total, False)
 
     @pl.when(lat > 0)
     def _():
         halo_copy.wait_send()
 
+    sums_pair_copy.wait_send()
     await_bytes(pair_stats, pair_send)
     await_bytes(peer_sums.at[pl.ds(0, chips - 1)], sum_send)
     await_bytes(received.at[pl.ds(0, chips - 1)], stat_send)
@@ -481,12 +526,16 @@
             vmem((planes, rows + SUB, columns), f32),
             vmem((levels, rows, columns), f32),
             vmem((blocks, fields * SUB, LANES), f32),
+            vmem((blocks, 2 * levels * SUB, LANES), f32),
+            vmem((blocks, LANES, LANES), jnp.bfloat16),
             vmem((planes + SUB, LANES), f32),
             vmem((planes + SUB, LANES), f32),
             vmem((parities, slots, packed, LANES), f32),
             vmem((slots, packed, LANES), f32),
             vmem((slots, packed, LANES), f32),
             vmem((chips, packed, LANES), f32),
+            vmem((parities, slots, SUB, LANES), f32),
+            vmem((slots, SUB, LANES), f32),
             vmem((slots, SUB, LANES), f32),
             vmem((chips, slots, SUB, LANES), f32),
             vmem((parities, slots, SUB, LANES), f32),
@@ -499,6 +548,8 @@
             dma,
             dma,
             dma((GROUPS,)),
+            dma,
+            dma,
             dma,
             dma,
             dma,

time: 12.8 us -> 12 us (0.938)
  Pallas kernels: 12 us -> 11.2 us
    pallas_call x1, Pallas kernels: 11.3 us -> 10.5 us  [shards(): pl.pallas_call(functools.partial(kernel, lat_devices, lon_devices, snapsh...]
where the time goes in v2:
time: 12 us; the launch traced here: 11.9 us
  Pallas kernels  11.2 us (93%)
  between operations  0.64 us (5%)
    pallas_call x1, Pallas kernels, shards(): pl.pallas_call(functools.partial(kernel, lat_devices, lon_devices, snapsh...  10.5 us
    pallas_call x1, Pallas kernels, shards(): pl.pallas_call(store, out_shape=(jax.ShapeDtypeStruct(eddy_shape, f32), j...  0.69 us

profile of v2, /device:TPU:0, one launch (start us, length us, event | category | flops | bytes accessed | tf_op | source)
XLA Modules:
  0.0 11.9 jit_solution(3824634593251587757)
XLA Ops:
  0.6 10.5 %heat_transport.1 = (f32[4,64,128]{2,1,0:T(8,128)S(1)}, f32[4,4,8,10]{3,2,1,0:T(8,128)S(1)}) custom-call(f32[40,64,128]{2,1,0:T(8,128)} %bitcast.3, f32[40,64,128]{2,1,0:T(8,128)} %bitcast.4, s32[64,128]{1,0:T(8,128)} %flag_hbm.1, s32[64,128]{1,0:T(8,128)} %floor_hbm.1, s32[64,128]{1,0:T(8,128)} %label_hbm.1), custom_call_target="tpu_custom_call" | custom-call | tf_op jit(solution)/shard_map/heat_transport/pallas_call | solution.py:517
  11.2 0.7 %store_results.1 = (f32[4,64,128]{2,1,0:T(8,128)}, f32[4,4,8,10]{3,2,1,0:T(8,128)}) custom-call(f32[4,64,128]{2,1,0:T(8,128)S(1)} %get-tuple-element.6.eddy_ref, f32[4,4,8,10]{3,2,1,0:T(8,128)S(1)} %get-tuple-element.7.transport_ref), custom_call_target="tpu_custom_call" | custom-call | tf_op jit(solution)/shard_map/store_results/pallas_call | solution.py:579

commit v3 on v2

--- a/solution.py
+++ b/solution.py
@@ -73,9 +73,6 @@
         pltpu.make_async_copy(column, columns.at[n], load_first).start()
     for b in range(blocks):
         warmth_copy(b).start()
-    for b in range(blocks):
-        flow_copy(b).start()
-
     barrier = pltpu.get_barrier_semaphore()
 
     def greet(d, carry):
@@ -89,6 +86,8 @@
         pl.semaphore_signal(barrier, inc=1, device_id=(lat + 1, me), device_id_type=MESH)
 
     lax.fori_loop(1, lon_devices, greet, 0)
+    for b in range(blocks):
+        flow_copy(b).start()
 
     halo_copy = pltpu.make_async_remote_copy(
         src_ref=halo_out, dst_ref=halo_in, send_sem=halo_send, recv_sem=halo_recv,

time: 12 us -> 11.8 us (0.983)
  Pallas kernels: 11.2 us -> 11 us
    pallas_call x1, Pallas kernels: 10.5 us -> 10.4 us  [shards(): pl.pallas_call(functools.partial(kernel, lat_devices, lon_devices, snapsh...]
where the time goes in v3:
time: 11.8 us; the launch traced here: 11.7 us
  Pallas kernels  11 us (93%)
  between operations  0.64 us (5%)
    pallas_call x1, Pallas kernels, shards(): pl.pallas_call(functools.partial(kernel, lat_devices, lon_devices, snapsh...  10.4 us
    pallas_call x1, Pallas kernels, shards(): pl.pallas_call(store, out_shape=(jax.ShapeDtypeStruct(eddy_shape, f32), j...  0.69 us

profile of v3, /device:TPU:0, one launch (start us, length us, event | category | flops | bytes accessed | tf_op | source)
XLA Modules:
  0.0 11.7 jit_solution(13307913976470056363)
XLA Ops:
  0.6 10.4 %heat_transport.1 = (f32[4,64,128]{2,1,0:T(8,128)S(1)}, f32[4,4,8,10]{3,2,1,0:T(8,128)S(1)}) custom-call(f32[40,64,128]{2,1,0:T(8,128)} %bitcast.3, f32[40,64,128]{2,1,0:T(8,128)} %bitcast.4, s32[64,128]{1,0:T(8,128)} %flag_hbm.1, s32[64,128]{1,0:T(8,128)} %floor_hbm.1, s32[64,128]{1,0:T(8,128)} %label_hbm.1), custom_call_target="tpu_custom_call" | custom-call | tf_op jit(solution)/shard_map/heat_transport/pallas_call | solution.py:516
  11.0 0.7 %store_results.1 = (f32[4,64,128]{2,1,0:T(8,128)}, f32[4,4,8,10]{3,2,1,0:T(8,128)}) custom-call(f32[4,64,128]{2,1,0:T(8,128)S(1)} %get-tuple-element.6.eddy_ref, f32[4,4,8,10]{3,2,1,0:T(8,128)S(1)} %get-tuple-element.7.transport_ref), custom_call_target="tpu_custom_call" | custom-call | tf_op jit(solution)/shard_map/store_results/pallas_call | solution.py:578

commit v4 on v3

--- a/solution.py
+++ b/solution.py
@@ -19,14 +19,14 @@
     lat_devices, lon_devices, snapshots, levels, share_rows,
     flow_hbm, warmth_hbm, flag_hbm, floor_hbm, label_hbm,
     eddy_ref, transport_ref,
-    columns, depth, flow, warmth, average, dots, mean_dots, members,
+    columns, depth, flow, warmth, average, members,
     halo_out, halo_in, stats, pair_stats, chip_stats, received, sums, pair_sums, chip_sums, peer_sums, all_sums,
     edge_sums, peer_edge, edge_stats, peer_edge_stats, edge_total, edge_stats_total,
     load_first, load_warmth, load_flow, halo_send, halo_recv,
     sums_pair_send, sums_pair_recv, pair_send, pair_recv, stat_send, stat_recv, sum_send, sum_recv, share_send, share_recv,
     edge_send, edge_recv, edge_stat_send, edge_stat_recv,
 ):
-    rows = flow.shape[1]
+    rows = flow.shape[0]
     blocks = rows // SUB
     last = blocks - 1
     half_blocks = blocks // GROUPS
@@ -35,7 +35,7 @@
     planes = snapshots * levels
     parities, slots, packed = stats.shape[:3]
     group_slots = slots // GROUPS
-    fields = dots.shape[1] // SUB
+    fields = packed * 3 // 2
     used = BASINS * SUB
     chips = lon_devices // 2
     lat = lax.axis_index("lat")
@@ -52,27 +52,23 @@
     def window(b):
         return pl.ds(b * SUB, SUB)
 
-    def flow_copy(b):
-        at = window(b)
-        return pltpu.make_async_copy(
-            flow_hbm.at[:, at, :], flow.at[:, at, :], load_flow.at[b // half_blocks]
-        )
-
-    def warmth_copy(b):
-        at = window(b)
-        sem = load_warmth if b else load_first
-        return pltpu.make_async_copy(warmth_hbm.at[:, at, :], warmth.at[:, at, :], sem)
+    group_rows = half_blocks * SUB
+
+    def load_rows(source, target, first, count, sem):
+        at = pl.ds(first, count)
+        for n in range(planes):
+            pltpu.make_async_copy(source.at[n, at, :], target.at[at, n, :], sem).start()
 
     def await_bytes(ref, sem):
         pltpu.make_async_copy(ref, ref, sem).wait()
 
-    def await_flow(g):
-        await_bytes(flow.at[:, pl.ds(0, half_blocks * SUB), :], load_flow.at[g])
-
     for n, column in enumerate((flag_hbm, floor_hbm, label_hbm)):
         pltpu.make_async_copy(column, columns.at[n], load_first).start()
-    for b in range(blocks):
-        warmth_copy(b).start()
+    pltpu.make_async_copy(warmth_hbm.at[:, 0, :], warmth.at[0], load_first).start()
+    for n in range(1, SUB):
+        pltpu.make_async_copy(warmth_hbm.at[:, n, :], warmth.at[n], load_warmth).start()
+    load_rows(warmth_hbm, warmth, SUB, rows - SUB, load_warmth)
+
     barrier = pltpu.get_barrier_semaphore()
 
     def greet(d, carry):
@@ -86,8 +82,8 @@
         pl.semaphore_signal(barrier, inc=1, device_id=(lat + 1, me), device_id_type=MESH)
 
     lax.fori_loop(1, lon_devices, greet, 0)
-    for b in range(blocks):
-        flow_copy(b).start()
+    for g in range(GROUPS):
+        load_rows(flow_hbm, flow, g * group_rows, group_rows, load_flow.at[g])
 
     halo_copy = pltpu.make_async_remote_copy(
         src_ref=halo_out, dst_ref=halo_in, send_sem=halo_send, recv_sem=halo_recv,
@@ -168,6 +164,8 @@
 
     def both_halves(x):
         return x + pltpu.roll(x, levels, 0)
+
+    level_of = lax.rem(sub, levels).astype(jnp.float32)
 
     def wet_cells(b):
         here = depth[window(b), :]
@@ -182,55 +180,64 @@
             (((1,), (1,)), ((), ())), preferred_element_type=jnp.float32,
         )
 
-    def by_row(ref, count):
+    def by_row(products, count):
+        products = products.reshape(SUB, count, LANES)
         row_of = lax.rem(lax.broadcasted_iota(jnp.int32, (count, LANES), 1), SUB)
-        zonal = ref[pl.ds(0, count, stride=SUB), :]
+        zonal = products[0]
         for j in range(1, SUB):
-            zonal = jnp.where(row_of == j, ref[pl.ds(j, count, stride=SUB), :], zonal)
+            zonal = jnp.where(row_of == j, products[j], zonal)
         return zonal
 
+    def wet_row(j):
+        limit = jnp.minimum(depth[pl.ds(j, 1), :], depth[pl.ds(j + 1, 1), :])
+        return (level_of < limit).astype(jnp.float32)
+
+    def tiles(x):
+        return x.reshape(planes // SUB, SUB, LANES)
+
     def block_means(b):
-        at = window(b)
-        wet = wet_cells(b)
-        here = jnp.sum(warmth[:, at, :].reshape(snapshots, levels, SUB, LANES), axis=0)
-        after = jnp.sum(
-            warmth[:, window(b + 1), :].reshape(snapshots, levels, SUB, LANES)[:, :, :1], axis=0
-        )
-        mean_warmth = (here + next_row(here, after)) * (0.5 / snapshots)
-        average[:, at, :] = mean_warmth
-        labels = label_ref[at, :]
+        labels = label_ref[window(b), :]
         member = jnp.concatenate(
             [(labels == n).astype(jnp.float32) for n in range(LANES // SUB)], axis=0
         ).astype(jnp.bfloat16)
         members[b] = member
-        values = jnp.concatenate([mean_warmth * wet, wet], axis=0).reshape(-1, LANES)
-        mean_dots[b] = split_dot(values, member)
-        sums[b % parities, b // parities] = by_row(mean_dots.at[b], 2 * levels)
-
-    def block_stats(b):
-        at = window(b)
-        wet = wet_cells(b)
-        velocity = flow[:, at, :].reshape(snapshots, levels, SUB, LANES)
-        here = warmth[:, at, :]
-        point = (0.5 * (here + next_row(here, warmth[:, window(b + 1), :]))).reshape(
-            snapshots, levels, SUB, LANES
-        )
-        mean_warmth = average[:, at, :]
-        mean_velocity = jnp.sum(velocity, axis=0) * (1.0 / snapshots)
-        cross = jnp.sum((velocity - mean_velocity) * (point - mean_warmth), axis=0) * (1.0 / snapshots)
-        values = jnp.concatenate(
+        sums_of_row = [
+            both_halves(jnp.sum(tiles(warmth[j]), axis=0)) for j in range(b * SUB, (b + 1) * SUB + 1)
+        ]
+        values = []
+        for n in range(SUB):
+            j = b * SUB + n
+            mean_warmth = (sums_of_row[n] + sums_of_row[n + 1]) * (0.5 / snapshots)
+            average[pl.ds(j * SUB, SUB), :] = mean_warmth
+            values.append(jnp.where(sub < levels, mean_warmth, 1.0) * wet_row(j))
+        products = split_dot(jnp.concatenate(values, axis=0), member)
+        sums[b % parities, b // parities] = by_row(products, SUB)
+
+    def row_values(velocity, point, mean_warmth, wet):
+        mean_velocity = both_halves(jnp.sum(velocity, axis=0)) * (1.0 / snapshots)
+        cross = both_halves(
+            jnp.sum((velocity - mean_velocity) * (point - 2.0 * mean_warmth), axis=0)
+        ) * (0.5 / snapshots)
+        return jnp.concatenate(
             [
-                (point * wet[None]).reshape(planes, SUB, LANES),
+                (point * (0.5 * wet)).reshape(planes, LANES),
                 wet,
-                wet,
-                (velocity * wet[None]).reshape(planes, SUB, LANES),
-                mean_velocity * mean_warmth * wet,
-                cross * wet,
+                (velocity * wet).reshape(planes, LANES),
+                jnp.where(sub < levels, mean_velocity * mean_warmth, cross) * wet,
             ],
             axis=0,
-        ).reshape(-1, LANES)
-        dots[b] = split_dot(values, members[b])
-        zonal = by_row(dots.at[b], fields)
+        )
+
+    def block_stats(b):
+        values = []
+        for j in range(b * SUB, (b + 1) * SUB):
+            values.append(
+                row_values(
+                    tiles(flow[j]), tiles(warmth[j] + warmth[j + 1]),
+                    average[pl.ds(j * SUB, SUB), :], wet_row(j),
+                )
+            )
+        zonal = by_row(split_dot(jnp.concatenate(values, axis=0), members[b]), fields)
         half = packed // 2
         rest = zonal[packed:]
         spare = lax.broadcasted_iota(jnp.int32, (half, LANES), 1) >= used
@@ -265,11 +272,11 @@
         each_chip(send_stats)
 
     await_bytes(columns, load_first)
-    await_bytes(warmth.at[:, window(0), :], load_first)
+    await_bytes(warmth.at[0], load_first)
     depth[pl.ds(0, rows), :] = (columns[0] * columns[1]).astype(jnp.float32)
     depth[pl.ds(rows, SUB), :] = jnp.zeros((SUB, LANES), jnp.float32)
-    warmth[:, rows, :] = jnp.zeros((planes, LANES), jnp.float32)
-    halo_out[pl.ds(0, planes), :] = warmth[:, 0, :]
+    warmth[rows] = jnp.zeros((planes, LANES), jnp.float32)
+    halo_out[pl.ds(0, planes), :] = warmth[0]
     halo_out[pl.ds(planes, SUB), :] = depth[pl.ds(0, SUB), :]
 
     pl.semaphore_wait(barrier, lon_devices - 1 + (lat > 0).astype(jnp.int32))
@@ -278,11 +285,11 @@
     def _():
         halo_copy.start()
 
-    await_bytes(warmth.at[:, pl.ds(0, last * SUB), :], load_warmth)
+    await_bytes(warmth.at[pl.ds(0, rows - 1)], load_warmth)
     for b in range(blocks):
         block_means(b)
     sums_pair_copy.start()
-    await_flow(0)
+    await_bytes(flow.at[pl.ds(0, group_rows)], load_flow.at[0])
     for b in range(half_blocks):
         block_stats(b)
     pair_copy(0).start()
@@ -290,7 +297,7 @@
     def _():
         send_sums()
 
-    await_flow(1)
+    await_bytes(flow.at[pl.ds(0, group_rows)], load_flow.at[1])
     for b in range(half_blocks, blocks):
         block_stats(b)
     pair_copy(1).start()
@@ -313,28 +320,12 @@
             lax.rem(column, SUB) == SUB - 1, label_ref[pl.ds(at, 1), :] == column // SUB
         )
         member = chosen.astype(jnp.float32).astype(jnp.bfloat16)
-        velocity = flow[:, at, :].reshape(planes // SUB, SUB, LANES)
-        mean_velocity = both_halves(jnp.sum(velocity, axis=0)) * (1.0 / snapshots)
-        here = warmth[:, at, :]
         halo_copy.wait_recv()
-        limit = jnp.minimum(depth[pl.ds(at, 1), :], halo_in[pl.ds(planes, 1), :])
-        wet = (lax.rem(sub, levels).astype(jnp.float32) < limit).astype(jnp.float32)
-        point = (0.5 * (here + halo_in[pl.ds(0, planes), :])).reshape(planes // SUB, SUB, LANES)
-        mean_warmth = both_halves(jnp.sum(point, axis=0)) * (1.0 / snapshots)
-        cross = both_halves(
-            jnp.sum((velocity - mean_velocity) * (point - mean_warmth), axis=0)
-        ) * (1.0 / snapshots)
-        average[:, at, :] = mean_warmth[:levels]
         depth[pl.ds(rows, SUB), :] = halo_in[pl.ds(planes, SUB), :]
-        values = jnp.concatenate(
-            [
-                (point * wet).reshape(planes, LANES),
-                wet,
-                (velocity * wet).reshape(planes, LANES),
-                jnp.where(sub < levels, mean_velocity * mean_warmth, cross) * wet,
-            ],
-            axis=0,
-        )
+        point = tiles(warmth[at] + halo_in[pl.ds(0, planes), :])
+        mean_warmth = both_halves(jnp.sum(point, axis=0)) * (0.5 / snapshots)
+        average[pl.ds(at * SUB, SUB), :] = mean_warmth
+        values = row_values(tiles(flow[at]), point, mean_warmth, wet_row(at))
         zonal = split_dot(values, member)
         edge_sums[...] = sums_of(zonal)
         each_peer(lambda to: edge_copy(to, me).start())
@@ -363,7 +354,8 @@
             cells = jnp.take_along_axis(
                 jnp.broadcast_to(bar[k : k + 1], (SUB, LANES)), index, axis=1
             )
-            eddy_ref[k, at, :] = wet[k] * (average[k, at, :] - cells)
+            mean_warmth = average[pl.ds(b * SUB * SUB + k, SUB, stride=SUB), :]
+            eddy_ref[k, at, :] = wet[k] * (mean_warmth - cells)
 
     def add_sums(d, total):
         source = lax.rem(chip + chips - d, chips)
@@ -521,11 +513,9 @@
         scratch_shapes=[
             vmem((3, rows, columns), i32),
             vmem((rows + SUB, columns), f32),
-            vmem((planes, rows, columns), f32),
-            vmem((planes, rows + SUB, columns), f32),
-            vmem((levels, rows, columns), f32),
-            vmem((blocks, fields * SUB, LANES), f32),
-            vmem((blocks, 2 * levels * SUB, LANES), f32),
+            vmem((rows, planes, columns), f32),
+            vmem((rows + 1, planes, columns), f32),
+            vmem((rows * SUB, columns), f32),
             vmem((blocks, LANES, LANES), jnp.bfloat16),
             vmem((planes + SUB, LANES), f32),
             vmem((planes + SUB, LANES), f32),

time: 11.8 us -> 11.7 us (level)
  Pallas kernels: 11 us -> 10.8 us
    pallas_call x1, Pallas kernels: 10.4 us -> 10.1 us  [shards(): pl.pallas_call(functools.partial(kernel, lat_devices, lon_devices, snapsh...]
where the time goes in v4:
time: 11.7 us; the launch traced here: 11.5 us
  Pallas kernels  10.8 us (92%)
  between operations  0.64 us (5%)
    pallas_call x1, Pallas kernels, shards(): pl.pallas_call(functools.partial(kernel, lat_devices, lon_devices, snapsh...  10.1 us
    pallas_call x1, Pallas kernels, shards(): pl.pallas_call(store, out_shape=(jax.ShapeDtypeStruct(eddy_shape, f32), j...  0.69 us

profile of v4, /device:TPU:0, one launch (start us, length us, event | category | flops | bytes accessed | tf_op | source)
XLA Modules:
  0.0 11.5 jit_solution(2591846916444759214)
XLA Ops:
  0.6 10.1 %heat_transport.1 = (f32[4,64,128]{2,1,0:T(8,128)S(1)}, f32[4,4,8,10]{3,2,1,0:T(8,128)S(1)}) custom-call(f32[40,64,128]{2,1,0:T(8,128)} %bitcast.3, f32[40,64,128]{2,1,0:T(8,128)} %bitcast.4, s32[64,128]{1,0:T(8,128)} %flag_hbm.1, s32[64,128]{1,0:T(8,128)} %floor_hbm.1, s32[64,128]{1,0:T(8,128)} %label_hbm.1), custom_call_target="tpu_custom_call" | custom-call | tf_op jit(solution)/shard_map/heat_transport/pallas_call | solution.py:508
  10.8 0.7 %store_results.1 = (f32[4,64,128]{2,1,0:T(8,128)}, f32[4,4,8,10]{3,2,1,0:T(8,128)}) custom-call(f32[4,64,128]{2,1,0:T(8,128)S(1)} %get-tuple-element.6.eddy_ref, f32[4,4,8,10]{3,2,1,0:T(8,128)S(1)} %get-tuple-element.7.transport_ref), custom_call_target="tpu_custom_call" | custom-call | tf_op jit(solution)/shard_map/store_results/pallas_call | solution.py:568
